TPU v7x, 8 devices: a whole 2x2x1 slice. The times are simulated.
8 devices in a mesh: dp: 1 (over z), sp: 8 (over y, x, core).
Axes of the slice: x: 2, y: 2, z: 1, core: 2. Of those that a mesh axis runs over, the one named last changes fastest.
Arguments:
- x_text: bfloat16 [12288, 4096], P(('dp', 'sp'))
- patches: bfloat16 [16, 576, 588], P(('dp', 'sp'))
- img_start: int32 [16], P('dp')
- w_patch: bfloat16 [588, 1024], replicated
- pos_table: bfloat16 [576, 1024], replicated
- vit_ln1: bfloat16 [1024], replicated
- w_vqkv: bfloat16 [1024, 3, 16, 64], replicated
- w_vout: bfloat16 [16, 64, 1024], replicated
- vit_ln2: bfloat16 [1024], replicated
- w_vfc1: bfloat16 [1024, 4096], replicated
- w_vfc2: bfloat16 [4096, 1024], replicated
- w_proj1: bfloat16 [1024, 4096], replicated
- w_proj2: bfloat16 [4096, 4096], replicated
- rms_attn: bfloat16 [4096], replicated
- w_query: bfloat16 [4096, 32, 128], replicated
- w_key: bfloat16 [4096, 32, 128], replicated
- w_value: bfloat16 [4096, 32, 128], replicated
- w_out: bfloat16 [32, 128, 4096], replicated
- rms_mlp: bfloat16 [4096], replicated
- w_gate: bfloat16 [4096, 11008], replicated
- w_up: bfloat16 [4096, 11008], replicated
- w_down: bfloat16 [11008, 4096], replicated
Outputs:
- output: bfloat16 [12288, 4096], P(('dp', 'sp'))
All inputs are finite; a program needn't handle non-finite values.
Results may differ from a plain program's by a relative error of at most 0.013174.
Values are sent between devices in bfloat16 or wider.
A program may use at most 2 GiB of HBM per device.

v0:
```python
import jax
import jax.numpy as jnp
from jax import lax
from jax.sharding import PartitionSpec as P

ROPE_BASE = 10000.0
RMS_EPS = 1e-6
LN_EPS = 1e-5


def layer_norm(values, gain):
    wide = values.astype(jnp.float32)
    row_mean = wide.mean(-1, keepdims=True)
    centered = wide - row_mean
    row_var = (centered * centered).mean(-1, keepdims=True)
    return (centered * lax.rsqrt(row_var + LN_EPS) * gain.astype(jnp.float32)).astype(jnp.bfloat16)


def rms_norm(values, gain):
    wide = values.astype(jnp.float32)
    mean_sq = (wide * wide).mean(-1, keepdims=True)
    return (wide * lax.rsqrt(mean_sq + RMS_EPS) * gain.astype(jnp.float32)).astype(jnp.bfloat16)


def apply_rope(values, positions):
    half_dim = values.shape[-1] // 2
    inv_freq = ROPE_BASE ** (-jnp.arange(half_dim).astype(jnp.float32) * 2.0 / values.shape[-1])
    angles = positions[:, None] * inv_freq[None, :]
    cosine = jnp.cos(angles)[:, None, :]
    sine = jnp.sin(angles)[:, None, :]
    first = values[..., :half_dim].astype(jnp.float32)
    second = values[..., half_dim:].astype(jnp.float32)
    return jnp.concatenate([first * cosine - second * sine, second * cosine + first * sine], axis=-1).astype(jnp.bfloat16)


def encode_images(pixels, w_patch, pos_table, vit_ln1, w_vqkv, w_vout, vit_ln2, value_a6, array_b6, w_proj1, w_proj2):
    embedded = (jnp.einsum('npc,cv->npv', pixels, w_patch, preferred_element_type=jnp.float32) + pos_table.astype(jnp.float32)).astype(jnp.bfloat16)
    normed = layer_norm(embedded, vit_ln1)
    qkv_all = jnp.einsum('npv,vthd->tnphd', normed, w_vqkv, preferred_element_type=jnp.float32).astype(jnp.bfloat16)
    scores = jnp.einsum('nqhd,nkhd->nhqk', qkv_all[0], qkv_all[1], preferred_element_type=jnp.float32) * w_vqkv.shape[3] ** -0.5
    attn_prob = jax.nn.softmax(scores, axis=-1).astype(jnp.bfloat16)
    context = jnp.einsum('nhqk,nkhd->nqhd', attn_prob, qkv_all[2], preferred_element_type=jnp.float32).astype(jnp.bfloat16)
    hidden = (embedded.astype(jnp.float32) + jnp.einsum('nqhd,hdv->nqv', context, w_vout, preferred_element_type=jnp.float32)).astype(jnp.bfloat16)
    normed_mlp = layer_norm(hidden, vit_ln2)
    hidden_act = jax.nn.gelu(jnp.einsum('npv,vf->npf', normed_mlp, value_a6, preferred_element_type=jnp.float32)).astype(jnp.bfloat16)
    vision = (hidden.astype(jnp.float32) + jnp.einsum('npf,fv->npv', hidden_act, array_b6, preferred_element_type=jnp.float32)).astype(jnp.bfloat16)
    proj_mid = jax.nn.gelu(jnp.einsum('npv,vd->npd', vision, w_proj1, preferred_element_type=jnp.float32)).astype(jnp.bfloat16)
    return jnp.einsum('npd,de->npe', proj_mid, w_proj2, preferred_element_type=jnp.float32).astype(jnp.bfloat16)


def stored_row(seq_pos, block_len, group_size, seq_dev):
    block_id = seq_pos // block_len
    first_half = block_id < group_size
    device = jnp.where(first_half, block_id, 2 * group_size - 1 - block_id)
    return device * seq_dev + jnp.where(first_half, 0, block_len) + seq_pos % block_len


def row_positions(device, block_len, group_size):
    offsets = jnp.arange(block_len)
    return jnp.concatenate([device * block_len + offsets, (2 * group_size - 1 - device) * block_len + offsets])


def attend_block(online_state, queries, q_pos, key_blk, value_blk, k_pos):
    run_max, run_sum, run_acc = online_state
    scores = jnp.einsum('qhgd,khd->hgqk', queries, key_blk, preferred_element_type=jnp.float32) * queries.shape[-1] ** -0.5
    allowed = k_pos[None, :] <= q_pos[:, None]
    scores = jnp.where(allowed, scores, -1e30)
    new_max = jnp.maximum(run_max, scores.max(axis=-1))
    exp_scores = jnp.where(allowed, jnp.exp(scores - new_max[..., None]), 0.0)
    factor = jnp.exp(run_max - new_max)
    new_sum = run_sum * factor + exp_scores.sum(axis=-1)
    new_acc = run_acc * factor[..., None] + jnp.einsum('hgqk,khd->hgqd', exp_scores.astype(jnp.bfloat16), value_blk, preferred_element_type=jnp.float32)
    return new_max, new_sum, new_acc


def decoder_layer(hidden, my_index, group_size, shift_pairs, rms_attn, w_query, w_key, w_value, w_out, rms_mlp, w_gate, w_up, w_down):
    seq_dev, width = hidden.shape
    block_len = seq_dev // 2
    kv_heads, head_dim = w_key.shape[1], w_key.shape[2]
    q_per_kv = w_query.shape[1] // kv_heads
    my_pos = row_positions(my_index, block_len, group_size)
    pos_wide = my_pos.astype(jnp.float32)
    normed = rms_norm(hidden, rms_attn)
    queries = apply_rope(jnp.einsum('sd,dhe->she', normed, w_query, preferred_element_type=jnp.float32).astype(jnp.bfloat16), pos_wide)
    key_rows = apply_rope(jnp.einsum('sd,dhe->she', normed, w_key, preferred_element_type=jnp.float32).astype(jnp.bfloat16), pos_wide)
    value_rows = jnp.einsum('sd,dhe->she', normed, w_value, preferred_element_type=jnp.float32).astype(jnp.bfloat16)
    q_halves = queries.reshape(2, block_len, kv_heads, q_per_kv, head_dim)
    pos_halves = my_pos.reshape(2, block_len)
    stat_shape = (kv_heads, q_per_kv, block_len)
    empty_state = (jnp.full(stat_shape, -jnp.inf, jnp.float32), jnp.zeros(stat_shape, jnp.float32), jnp.zeros(stat_shape + (head_dim,), jnp.float32))
    states = tuple(attend_block(empty_state, q_halves[half_idx], pos_halves[half_idx], key_rows, value_rows, my_pos) for half_idx in range(2))

    def kv_step(step_idx, carry):
        key_blk, value_blk, prev_states = carry
        key_blk = lax.ppermute(key_blk, 'sp', shift_pairs)
        value_blk = lax.ppermute(value_blk, 'sp', shift_pairs)
        k_pos = row_positions((my_index - step_idx) % group_size, block_len, group_size)
        return key_blk, value_blk, tuple(attend_block(prev_states[half_idx], q_halves[half_idx], pos_halves[half_idx], key_blk, value_blk, k_pos) for half_idx in range(2))

    final = lax.fori_loop(1, group_size, kv_step, (key_rows, value_rows, states))
    w_out_grouped = w_out.reshape(kv_heads, q_per_kv, head_dim, width)
    halves = []
    for half_idx in range(2):
        context = (final[2][half_idx][2] / final[2][half_idx][1][..., None]).astype(jnp.bfloat16)
        halves.append(jnp.einsum('hgqd,hgde->qe', context, w_out_grouped, preferred_element_type=jnp.float32))
    attn_out = jnp.concatenate(halves, axis=0)
    mid_rows = (hidden.astype(jnp.float32) + attn_out).astype(jnp.bfloat16)
    normed_mlp = rms_norm(mid_rows, rms_mlp)
    gate_act = jnp.dot(normed_mlp, w_gate, preferred_element_type=jnp.float32)
    up_proj = jnp.dot(normed_mlp, w_up, preferred_element_type=jnp.float32)
    mixed = (jax.nn.silu(gate_act) * up_proj).astype(jnp.bfloat16)
    return (mid_rows.astype(jnp.float32) + jnp.dot(mixed, w_down, preferred_element_type=jnp.float32)).astype(jnp.bfloat16)


def solution(mesh):
    group_size = mesh.shape['sp']
    shift_pairs = [(device, (device + 1) % group_size) for device in range(group_size)]

    def local_program(x_rows, pixels, starts, w_patch, pos_table, vit_ln1, w_vqkv, w_vout, vit_ln2, value_a6, array_b6, w_proj1, w_proj2, rms_attn, w_query, w_key, w_value, w_out, rms_mlp, w_gate, w_up, w_down):
        my_index = lax.axis_index('sp')
        seq_dev, width = x_rows.shape
        block_len = seq_dev // 2
        img_count, patch_len = pixels.shape[0], pixels.shape[1]
        slot_cap = -(-img_count // group_size)
        img_rows = encode_images(pixels, w_patch, pos_table, vit_ln1, w_vqkv, w_vout, vit_ln2, value_a6, array_b6, w_proj1, w_proj2)
        my_starts = lax.dynamic_slice(starts, (my_index * img_count,), (img_count,))
        target = stored_row(my_starts, block_len, group_size, seq_dev)
        dest_dev = target // seq_dev
        local_row = target % seq_dev
        order = jnp.arange(img_count)
        dest_rank = jnp.sum((dest_dev[None, :] == dest_dev[:, None]) & (order[None, :] < order[:, None]), axis=1).astype(jnp.int32)
        slot_of = dest_dev * slot_cap + dest_rank
        match = jnp.arange(group_size * slot_cap)[:, None] == slot_of[None, :]
        send_start = (jnp.sum(jnp.where(match, local_row[None, :] + 1, 0), axis=1) - 1).astype(jnp.int32)

        def fill(image_idx, send_rows):
            return lax.dynamic_update_slice(send_rows, lax.dynamic_slice_in_dim(img_rows, image_idx, 1, axis=0), (slot_of[image_idx], 0, 0))

        send_rows = lax.fori_loop(0, img_count, fill, jnp.zeros((group_size * slot_cap, patch_len, width), jnp.bfloat16))
        recv_rows = lax.all_to_all(send_rows, 'sp', 0, 0, tiled=True)
        recv_start = lax.all_to_all(send_start, 'sp', 0, 0, tiled=True)

        def place(slot_idx, hidden):
            start_row = recv_start[slot_idx]
            is_valid = start_row >= 0
            safe_row = jnp.where(is_valid, start_row, 0)
            current = lax.dynamic_slice(hidden, (safe_row, 0), (patch_len, width))
            incoming = lax.dynamic_index_in_dim(recv_rows, slot_idx, axis=0, keepdims=False)
            return lax.dynamic_update_slice(hidden, jnp.where(is_valid, incoming, current), (safe_row, 0))

        hidden = lax.fori_loop(0, group_size * slot_cap, place, x_rows)
        return decoder_layer(hidden, my_index, group_size, shift_pairs, rms_attn, w_query, w_key, w_value, w_out, rms_mlp, w_gate, w_up, w_down)

    row_spec = P(('dp', 'sp'), None)
    in_specs = (row_spec, P(('dp', 'sp'), None, None), P('dp')) + (P(),) * 19
    return jax.shard_map(local_program, mesh=mesh, in_specs=in_specs, out_specs=row_spec, check_vma=False)
```

profile of v0, /device:TPU:0, one launch (start us, length us, event | category | flops | bytes accessed | tf_op | source)
XLA Modules:
  0.0 5682.8 jit_solution(14657803800425176527)
XLA Ops:
  301.7 316.4 %all-to-all-done.1 = bf16[8,576,4096]{2,1,0:T(8,128)(2,1)} async-done(((bf16[8,576,4096]{2,1,0:T(8,128)(2,1)}), bf16[8,576,4096]{2,1,0:T(8,128)(2,1)}, u32[]{:S(2)}, u32[]{:S(2)}) %all-to-all-start.1) | async-done | bytes 37748768 | tf_op jit(solution)/shard_map/all_to_all | solution.py:140
  618.1 267.9 %while.56 = (s32[]{:T(128)}, bf16[1536,4096]{1,0:T(8,128)(2,1)}, s32[8]{0:T(128)S(1)}, bf16[8,576,4096]{2,1,0:T(8,128)(2,1)}, s32[]{:T(128)}, /*index=5*/s32[]{:T(128)}, s32[]{:T(128)}) while((s32[]{:T(128)}, bf16[1536,4096]{1,0:T(8,128)(2,1)}, s32[8]{0:T(128)S(1)}, bf16[8,576,4096]{2,1,0:T(8,128)(2,1)}, s32[]{:T(128)}, ...), condition=%wide.region_11.12_spmd, body=%wide.region_10.11_spmd.sunk | while | flops 2359303 | bytes 23593124 | solution.py:151
  893.1 62.7 %fusion.178 = f32[1536,4096]{0,1} fusion(bf16[4096,4096]{0,1:T(8,128)(2,1)} %bitcast.338, bf16[1536,4096]{1,0:T(8,128)(2,1)} %get-tuple-element.454, f32[4096]{0:T(1024)S(1)} %convert_element_type.185, f32[1536]{0:T(1024)S(1)} %add_rsqrt_fusion.1), kind=kOutput, calls=%fused_computation.234 | convolution fusion | flops 51564773376 | bytes 71325696
  955.9 62.7 %fusion.181 = f32[1536,4096]{0,1} fusion(bf16[4096,4096]{0,1:T(8,128)(2,1)} %bitcast.337, bf16[1536,4096]{1,0:T(8,128)(2,1)} %get-tuple-element.454, f32[4096]{0:T(1024)S(1)} %convert_element_type.185, f32[1536]{0:T(1024)S(1)} %add_rsqrt_fusion.1), kind=kOutput, calls=%fused_computation.235 | convolution fusion | flops 51564773376 | bytes 71325696
  1123.1 62.1 %fusion.80 = bf16[1536,32,128]{2,0,1:T(8,128)(2,1)} fusion(bf16[4096,32,128]{2,1,0:T(8,128)(2,1)} %param.44, bf16[1536,4096]{1,0:T(8,128)(2,1)} %get-tuple-element.454, f32[4096]{0:T(1024)S(1)} %convert_element_type.185, f32[1536]{0:T(1024)S(1)} %add_rsqrt_fusion.1), kind=kOutput, calls=%fused_computation.115 | convolution fusion | flops 51571064832 | bytes 58742784 | tf_op jit(solution)/shard_map/sd,dhe->she/dot_general | solution.py:86
  1424.7 64.8 %add_bitcast_fusion = f32[32,1,768,128]{3,2,0,1:T(8,128)} fusion(f32[32,768]{1,0:T(8,128)S(1)} %exponential_multiply_fusion, bf16[1536,32,128]{2,0,1:T(8,128)(2,1)} %fusion.80, f32[32,1536,768]{2,1,0:T(8,128)} %get-tuple-element.586, f32[32,768]{1,0:T(8,128)} %get-tuple-element.585, pred[768,1536]{0,1:T(8,128)(4,1)S(1)} %copy-done.5), kind=kOutput, calls=%fused_computation.131 | convolution fusion | flops 9855565824 | bytes 177537024 | tf_op jit(solution)/shard_map/hgqk,khd->hgqd/dot_general | solution.py:72
  1489.5 65.1 %add_bitcast_fusion.1 = f32[32,1,768,128]{3,2,0,1:T(8,128)} fusion(f32[32,768]{1,0:T(8,128)S(1)} %exponential_multiply_fusion.1, bf16[1536,32,128]{2,0,1:T(8,128)(2,1)} %fusion.80, f32[32,1536,768]{2,1,0:T(8,128)} %get-tuple-element.584, f32[32,768]{1,0:T(8,128)S(1)} %get-tuple-element.583, pred[768,1536]{0,1:T(8,128)(4,1)S(1)} %copy-done.4), kind=kOutput, calls=%fused_computation.132 | convolution fusion | flops 9855565824 | bytes 177537024 | tf_op jit(solution)/shard_map/hgqk,khd->hgqd/dot_general | solution.py:72
  1570.5 3527.3 %while.57 = (s32[]{:T(128)}, bf16[1536,32,128]{2,0,1:T(8,128)(2,1)}, bf16[1536,32,128]{2,0,1:T(8,128)(2,1)}, f32[32,1,768]{2,0,1:T(8,128)}, f32[32,1,768]{2,0,1:...) while((s32[]{:T(128)}, ...), condition=%wide.region_22.23_spmd, body=%wide.region_17.22_spmd.sunk | while | flops 39651266560 | bytes 1185614208 | solution.py:100
  1572.5 136.9 %collective-permute-done = bf16[1536,32,128]{2,0,1:T(8,128)(2,1)} collective-permute-done((bf16[1536,32,128]{2,0,1:T(8,128)(2,1)}, bf16[1536,32,128]{2,0,1:T(8,128)(2,1)}, u32[]{:S(2)}, u32[]{:S(2)}) %collective-permute-start) | collective-permute-done | bytes 12582944 | tf_op jit(solution)/shard_map/while/body/eval_jaxpr/ppermute | solution.py:95
  1940.9 66.9 %bitcast_add_fusion.11 = f32[32,1,768,128]{3,2,0,1:T(8,128)} fusion(f32[32,1,768,128]{3,2,0,1:T(8,128)} %get-tuple-element.808, f32[32,768]{1,0:T(8,128)S(1)} %copy-done.11, bf16[1536,32,128]{2,0,1:T(8,128)(2,1)} %collective-permute-done.1, f32[32,1536,768]{2,1,0:T(8,128)} %get-tuple-element.732, f32[32,768]{1,0:T(8,128)S(1)} %bitcast.334, ...), kind=kOutput, calls=%fused_computation.18.clone.2 | convolution fusion | flops 9858711552 | bytes 190119936 | tf_op jit(solution)/shard_map/while/body/eval_jaxpr/hgqk,khd->hgqd/dot_general | solution.py:72
  2007.9 66.7 %bitcast_add_fusion.10 = f32[32,1,768,128]{3,2,0,1:T(8,128)} fusion(f32[32,1,768,128]{3,2,0,1:T(8,128)} %get-tuple-element.805, f32[32,768]{1,0:T(8,128)S(1)} %copy-done.12, bf16[1536,32,128]{2,0,1:T(8,128)(2,1)} %collective-permute-done.1, f32[32,1536,768]{2,1,0:T(8,128)} %get-tuple-element.735, f32[32,768]{1,0:T(8,128)S(1)} %bitcast.336, ...), kind=kOutput, calls=%fused_computation.19.clone.1 | convolution fusion | flops 9858711552 | bytes 190119936 | tf_op jit(solution)/shard_map/while/body/eval_jaxpr/hgqk,khd->hgqd/dot_general | solution.py:72
  2076.3 137.0 %collective-permute-done = bf16[1536,32,128]{2,0,1:T(8,128)(2,1)} collective-permute-done((bf16[1536,32,128]{2,0,1:T(8,128)(2,1)}, bf16[1536,32,128]{2,0,1:T(8,128)(2,1)}, u32[]{:S(2)}, u32[]{:S(2)}) %collective-permute-start) | collective-permute-done | bytes 12582944 | tf_op jit(solution)/shard_map/while/body/eval_jaxpr/ppermute | solution.py:95
  2444.7 66.9 %bitcast_add_fusion.11 = f32[32,1,768,128]{3,2,0,1:T(8,128)} fusion(f32[32,1,768,128]{3,2,0,1:T(8,128)} %get-tuple-element.808, f32[32,768]{1,0:T(8,128)S(1)} %copy-done.11, bf16[1536,32,128]{2,0,1:T(8,128)(2,1)} %collective-permute-done.1, f32[32,1536,768]{2,1,0:T(8,128)} %get-tuple-element.732, f32[32,768]{1,0:T(8,128)S(1)} %bitcast.334, ...), kind=kOutput, calls=%fused_computation.18.clone.2 | convolution fusion | flops 9858711552 | bytes 190119936 | tf_op jit(solution)/shard_map/while/body/eval_jaxpr/hgqk,khd->hgqd/dot_general | solution.py:72
  2511.7 66.7 %bitcast_add_fusion.10 = f32[32,1,768,128]{3,2,0,1:T(8,128)} fusion(f32[32,1,768,128]{3,2,0,1:T(8,128)} %get-tuple-element.805, f32[32,768]{1,0:T(8,128)S(1)} %copy-done.12, bf16[1536,32,128]{2,0,1:T(8,128)(2,1)} %collective-permute-done.1, f32[32,1536,768]{2,1,0:T(8,128)} %get-tuple-element.735, f32[32,768]{1,0:T(8,128)S(1)} %bitcast.336, ...), kind=kOutput, calls=%fused_computation.19.clone.1 | convolution fusion | flops 9858711552 | bytes 190119936 | tf_op jit(solution)/shard_map/while/body/eval_jaxpr/hgqk,khd->hgqd/dot_general | solution.py:72
  2580.1 137.0 %collective-permute-done = bf16[1536,32,128]{2,0,1:T(8,128)(2,1)} collective-permute-done((bf16[1536,32,128]{2,0,1:T(8,128)(2,1)}, bf16[1536,32,128]{2,0,1:T(8,128)(2,1)}, u32[]{:S(2)}, u32[]{:S(2)}) %collective-permute-start) | collective-permute-done | bytes 12582944 | tf_op jit(solution)/shard_map/while/body/eval_jaxpr/ppermute | solution.py:95
  2948.6 66.9 %bitcast_add_fusion.11 = f32[32,1,768,128]{3,2,0,1:T(8,128)} fusion(f32[32,1,768,128]{3,2,0,1:T(8,128)} %get-tuple-element.808, f32[32,768]{1,0:T(8,128)S(1)} %copy-done.11, bf16[1536,32,128]{2,0,1:T(8,128)(2,1)} %collective-permute-done.1, f32[32,1536,768]{2,1,0:T(8,128)} %get-tuple-element.732, f32[32,768]{1,0:T(8,128)S(1)} %bitcast.334, ...), kind=kOutput, calls=%fused_computation.18.clone.2 | convolution fusion | flops 9858711552 | bytes 190119936 | tf_op jit(solution)/shard_map/while/body/eval_jaxpr/hgqk,khd->hgqd/dot_general | solution.py:72
  3015.5 66.7 %bitcast_add_fusion.10 = f32[32,1,768,128]{3,2,0,1:T(8,128)} fusion(f32[32,1,768,128]{3,2,0,1:T(8,128)} %get-tuple-element.805, f32[32,768]{1,0:T(8,128)S(1)} %copy-done.12, bf16[1536,32,128]{2,0,1:T(8,128)(2,1)} %collective-permute-done.1, f32[32,1536,768]{2,1,0:T(8,128)} %get-tuple-element.735, f32[32,768]{1,0:T(8,128)S(1)} %bitcast.336, ...), kind=kOutput, calls=%fused_computation.19.clone.1 | convolution fusion | flops 9858711552 | bytes 190119936 | tf_op jit(solution)/shard_map/while/body/eval_jaxpr/hgqk,khd->hgqd/dot_general | solution.py:72
  3083.9 137.0 %collective-permute-done = bf16[1536,32,128]{2,0,1:T(8,128)(2,1)} collective-permute-done((bf16[1536,32,128]{2,0,1:T(8,128)(2,1)}, bf16[1536,32,128]{2,0,1:T(8,128)(2,1)}, u32[]{:S(2)}, u32[]{:S(2)}) %collective-permute-start) | collective-permute-done | bytes 12582944 | tf_op jit(solution)/shard_map/while/body/eval_jaxpr/ppermute | solution.py:95
  3452.4 66.9 %bitcast_add_fusion.11 = f32[32,1,768,128]{3,2,0,1:T(8,128)} fusion(f32[32,1,768,128]{3,2,0,1:T(8,128)} %get-tuple-element.808, f32[32,768]{1,0:T(8,128)S(1)} %copy-done.11, bf16[1536,32,128]{2,0,1:T(8,128)(2,1)} %collective-permute-done.1, f32[32,1536,768]{2,1,0:T(8,128)} %get-tuple-element.732, f32[32,768]{1,0:T(8,128)S(1)} %bitcast.334, ...), kind=kOutput, calls=%fused_computation.18.clone.2 | convolution fusion | flops 9858711552 | bytes 190119936 | tf_op jit(solution)/shard_map/while/body/eval_jaxpr/hgqk,khd->hgqd/dot_general | solution.py:72
  3519.3 66.7 %bitcast_add_fusion.10 = f32[32,1,768,128]{3,2,0,1:T(8,128)} fusion(f32[32,1,768,128]{3,2,0,1:T(8,128)} %get-tuple-element.805, f32[32,768]{1,0:T(8,128)S(1)} %copy-done.12, bf16[1536,32,128]{2,0,1:T(8,128)(2,1)} %collective-permute-done.1, f32[32,1536,768]{2,1,0:T(8,128)} %get-tuple-element.735, f32[32,768]{1,0:T(8,128)S(1)} %bitcast.336, ...), kind=kOutput, calls=%fused_computation.19.clone.1 | convolution fusion | flops 9858711552 | bytes 190119936 | tf_op jit(solution)/shard_map/while/body/eval_jaxpr/hgqk,khd->hgqd/dot_general | solution.py:72
  3587.7 137.0 %collective-permute-done = bf16[1536,32,128]{2,0,1:T(8,128)(2,1)} collective-permute-done((bf16[1536,32,128]{2,0,1:T(8,128)(2,1)}, bf16[1536,32,128]{2,0,1:T(8,128)(2,1)}, u32[]{:S(2)}, u32[]{:S(2)}) %collective-permute-start) | collective-permute-done | bytes 12582944 | tf_op jit(solution)/shard_map/while/body/eval_jaxpr/ppermute | solution.py:95
  3956.2 66.9 %bitcast_add_fusion.11 = f32[32,1,768,128]{3,2,0,1:T(8,128)} fusion(f32[32,1,768,128]{3,2,0,1:T(8,128)} %get-tuple-element.808, f32[32,768]{1,0:T(8,128)S(1)} %copy-done.11, bf16[1536,32,128]{2,0,1:T(8,128)(2,1)} %collective-permute-done.1, f32[32,1536,768]{2,1,0:T(8,128)} %get-tuple-element.732, f32[32,768]{1,0:T(8,128)S(1)} %bitcast.334, ...), kind=kOutput, calls=%fused_computation.18.clone.2 | convolution fusion | flops 9858711552 | bytes 190119936 | tf_op jit(solution)/shard_map/while/body/eval_jaxpr/hgqk,khd->hgqd/dot_general | solution.py:72
  4023.1 66.7 %bitcast_add_fusion.10 = f32[32,1,768,128]{3,2,0,1:T(8,128)} fusion(f32[32,1,768,128]{3,2,0,1:T(8,128)} %get-tuple-element.805, f32[32,768]{1,0:T(8,128)S(1)} %copy-done.12, bf16[1536,32,128]{2,0,1:T(8,128)(2,1)} %collective-permute-done.1, f32[32,1536,768]{2,1,0:T(8,128)} %get-tuple-element.735, f32[32,768]{1,0:T(8,128)S(1)} %bitcast.336, ...), kind=kOutput, calls=%fused_computation.19.clone.1 | convolution fusion | flops 9858711552 | bytes 190119936 | tf_op jit(solution)/shard_map/while/body/eval_jaxpr/hgqk,khd->hgqd/dot_general | solution.py:72
  4091.6 137.0 %collective-permute-done = bf16[1536,32,128]{2,0,1:T(8,128)(2,1)} collective-permute-done((bf16[1536,32,128]{2,0,1:T(8,128)(2,1)}, bf16[1536,32,128]{2,0,1:T(8,128)(2,1)}, u32[]{:S(2)}, u32[]{:S(2)}) %collective-permute-start) | collective-permute-done | bytes 12582944 | tf_op jit(solution)/shard_map/while/body/eval_jaxpr/ppermute | solution.py:95
  4460.0 66.9 %bitcast_add_fusion.11 = f32[32,1,768,128]{3,2,0,1:T(8,128)} fusion(f32[32,1,768,128]{3,2,0,1:T(8,128)} %get-tuple-element.808, f32[32,768]{1,0:T(8,128)S(1)} %copy-done.11, bf16[1536,32,128]{2,0,1:T(8,128)(2,1)} %collective-permute-done.1, f32[32,1536,768]{2,1,0:T(8,128)} %get-tuple-element.732, f32[32,768]{1,0:T(8,128)S(1)} %bitcast.334, ...), kind=kOutput, calls=%fused_computation.18.clone.2 | convolution fusion | flops 9858711552 | bytes 190119936 | tf_op jit(solution)/shard_map/while/body/eval_jaxpr/hgqk,khd->hgqd/dot_general | solution.py:72
  4527.0 66.7 %bitcast_add_fusion.10 = f32[32,1,768,128]{3,2,0,1:T(8,128)} fusion(f32[32,1,768,128]{3,2,0,1:T(8,128)} %get-tuple-element.805, f32[32,768]{1,0:T(8,128)S(1)} %copy-done.12, bf16[1536,32,128]{2,0,1:T(8,128)(2,1)} %collective-permute-done.1, f32[32,1536,768]{2,1,0:T(8,128)} %get-tuple-element.735, f32[32,768]{1,0:T(8,128)S(1)} %bitcast.336, ...), kind=kOutput, calls=%fused_computation.19.clone.1 | convolution fusion | flops 9858711552 | bytes 190119936 | tf_op jit(solution)/shard_map/while/body/eval_jaxpr/hgqk,khd->hgqd/dot_general | solution.py:72
  4595.4 137.0 %collective-permute-done = bf16[1536,32,128]{2,0,1:T(8,128)(2,1)} collective-permute-done((bf16[1536,32,128]{2,0,1:T(8,128)(2,1)}, bf16[1536,32,128]{2,0,1:T(8,128)(2,1)}, u32[]{:S(2)}, u32[]{:S(2)}) %collective-permute-start) | collective-permute-done | bytes 12582944 | tf_op jit(solution)/shard_map/while/body/eval_jaxpr/ppermute | solution.py:95
  4963.8 66.9 %bitcast_add_fusion.11 = f32[32,1,768,128]{3,2,0,1:T(8,128)} fusion(f32[32,1,768,128]{3,2,0,1:T(8,128)} %get-tuple-element.808, f32[32,768]{1,0:T(8,128)S(1)} %copy-done.11, bf16[1536,32,128]{2,0,1:T(8,128)(2,1)} %collective-permute-done.1, f32[32,1536,768]{2,1,0:T(8,128)} %get-tuple-element.732, f32[32,768]{1,0:T(8,128)S(1)} %bitcast.334, ...), kind=kOutput, calls=%fused_computation.18.clone.2 | convolution fusion | flops 9858711552 | bytes 190119936 | tf_op jit(solution)/shard_map/while/body/eval_jaxpr/hgqk,khd->hgqd/dot_general | solution.py:72
  5030.8 66.7 %bitcast_add_fusion.10 = f32[32,1,768,128]{3,2,0,1:T(8,128)} fusion(f32[32,1,768,128]{3,2,0,1:T(8,128)} %get-tuple-element.805, f32[32,768]{1,0:T(8,128)S(1)} %copy-done.12, bf16[1536,32,128]{2,0,1:T(8,128)(2,1)} %collective-permute-done.1, f32[32,1536,768]{2,1,0:T(8,128)} %get-tuple-element.735, f32[32,768]{1,0:T(8,128)S(1)} %bitcast.336, ...), kind=kOutput, calls=%fused_computation.19.clone.1 | convolution fusion | flops 9858711552 | bytes 190119936 | tf_op jit(solution)/shard_map/while/body/eval_jaxpr/hgqk,khd->hgqd/dot_general | solution.py:72
  5194.9 156.3 %fusion.129 = f32[1536,11008]{1,0:T(8,128)} fusion(bf16[4096,11008]{1,0:T(8,128)(2,1)} %param.47, bf16[1536,4096]{1,0:T(8,128)(2,1)} %get-tuple-element.554, f32[4096]{0:T(1024)S(1)} %copy-done.19, f32[1536]{0:T(1024)S(1)} %add_rsqrt_fusion), kind=kOutput, calls=%fused_computation.170 | convolution fusion | flops 138537861120 | bytes 170416128 | tf_op jit(solution)/shard_map/dot_general | solution.py:109
  5351.2 170.1 %multiply_convert_fusion = bf16[1536,11008]{1,0:T(8,128)(2,1)} fusion(f32[1536,11008]{1,0:T(8,128)} %fusion.129, bf16[4096,11008]{1,0:T(8,128)(2,1)} %param.48, bf16[1536,4096]{1,0:T(8,128)(2,1)} %get-tuple-element.554, f32[4096]{0:T(1024)S(1)} %copy-done.19, f32[1536]{0:T(1024)S(1)} %add_rsqrt_fusion), kind=kOutput, calls=%fused_computation.64 | convolution fusion | flops 138639310848 | bytes 204232704 | tf_op jit(solution)/shard_map/dot_general | solution.py:110
  5521.2 161.3 %fusion.61 = bf16[1536,4096]{1,0:T(8,128)(2,1)} fusion(bf16[1536,4096]{1,0:T(8,128)(2,1)} %get-tuple-element.554, bf16[1536,11008]{1,0:T(8,128)(2,1)} %multiply_convert_fusion, bf16[11008,4096]{1,0:T(8,128)(2,1)} %param.49), kind=kOutput, calls=%fused_computation.88 | convolution fusion | flops 138531569664 | bytes 149159936 | tf_op jit(solution)/shard_map/dot_general | solution.py:112
  (375 shorter events, 2667.7 us)
Async XLA Ops:
  12.4 190.3 %all-to-all-start = ((s32[8,1,1]{2,1,0:T(1,128)}), s32[8,1,1]{2,1,0:T(1,128)}, u32[]{:S(2)}, u32[]{:S(2)}) async-start(s32[8,1,1]{2,1,0:T(1,128)} %copy.70), calls=%async_computation | async-start | bytes 8192 | tf_op jit(solution)/shard_map/all_to_all | solution.py:141
  202.7 415.4 %all-to-all-start.1 = ((bf16[8,576,4096]{2,1,0:T(8,128)(2,1)}), bf16[8,576,4096]{2,1,0:T(8,128)(2,1)}, u32[]{:S(2)}, u32[]{:S(2)}) async-start(bf16[8,576,4096]{2,1,0:T(8,128)(2,1)} %get-tuple-element.453), calls=%async_computation.1 | async-start | bytes 75497472 | tf_op jit(solution)/shard_map/all_to_all | solution.py:140
  1377.8 111.7 %copy-start.2 = (f32[32,768]{1,0:T(8,128)}, f32[32,768]{1,0:T(8,128)S(1)}, u32[]{:S(2)}) copy-start(f32[32,768]{1,0:T(8,128)S(1)} %get-tuple-element.583) | copy-start | bytes 294916
  1570.7 138.7 %collective-permute-start = (bf16[1536,32,128]{2,0,1:T(8,128)(2,1)}, bf16[1536,32,128]{2,0,1:T(8,128)(2,1)}, u32[]{:S(2)}, u32[]{:S(2)}) collective-permute-start(bf16[1536,32,128]{2,0,1:T(8,128)(2,1)} %get-tuple-element.801), channel_id=1, source_target_pairs={{0,1},{1,2},{2,3},{3,4},{4,5},{5,6},{6,7},{7,0}} | collective-permute-start | bytes 37748744 | tf_op jit(solution)/shard_map/while/body/eval_jaxpr/ppermute | solution.py:95
  1570.7 358.9 %collective-permute-start.1 = (bf16[1536,32,128]{2,0,1:T(8,128)(2,1)}, bf16[1536,32,128]{2,0,1:T(8,128)(2,1)}, u32[]{:S(2)}, u32[]{:S(2)}) collective-permute-start(bf16[1536,32,128]{2,0,1:T(8,128)(2,1)} %get-tuple-element.802), channel_id=1, source_target_pairs={{0,1},{1,2},{2,3},{3,4},{4,5},{5,6},{6,7},{7,0}} | collective-permute-start | bytes 37748744 | tf_op jit(solution)/shard_map/while/body/eval_jaxpr/ppermute | solution.py:96
  1940.9 66.9 %copy-start.12 = (f32[32,768]{1,0:T(8,128)S(1)}, f32[32,768]{1,0:T(8,128)}, u32[]{:S(2)}) copy-start(f32[32,768]{1,0:T(8,128)} %get-tuple-element.737) | copy-start | bytes 294916 | tf_op jit(solution)/shard_map/while
  2007.9 66.7 %copy-start.18 = (s32[2,768]{1,0:T(2,128)S(1)}, s32[2,768]{1,0:T(2,128)}, u32[]{:S(2)}) copy-start(s32[2,768]{1,0:T(2,128)} %get-tuple-element.857) | copy-start | bytes 18436 | tf_op jit(solution)/shard_map/while
  2074.5 138.7 %collective-permute-start = (bf16[1536,32,128]{2,0,1:T(8,128)(2,1)}, bf16[1536,32,128]{2,0,1:T(8,128)(2,1)}, u32[]{:S(2)}, u32[]{:S(2)}) collective-permute-start(bf16[1536,32,128]{2,0,1:T(8,128)(2,1)} %get-tuple-element.801), channel_id=1, source_target_pairs={{0,1},{1,2},{2,3},{3,4},{4,5},{5,6},{6,7},{7,0}} | collective-permute-start | bytes 37748744 | tf_op jit(solution)/shard_map/while/body/eval_jaxpr/ppermute | solution.py:95
  2074.5 358.9 %collective-permute-start.1 = (bf16[1536,32,128]{2,0,1:T(8,128)(2,1)}, bf16[1536,32,128]{2,0,1:T(8,128)(2,1)}, u32[]{:S(2)}, u32[]{:S(2)}) collective-permute-start(bf16[1536,32,128]{2,0,1:T(8,128)(2,1)} %get-tuple-element.802), channel_id=1, source_target_pairs={{0,1},{1,2},{2,3},{3,4},{4,5},{5,6},{6,7},{7,0}} | collective-permute-start | bytes 37748744 | tf_op jit(solution)/shard_map/while/body/eval_jaxpr/ppermute | solution.py:96
  2444.7 66.9 %copy-start.12 = (f32[32,768]{1,0:T(8,128)S(1)}, f32[32,768]{1,0:T(8,128)}, u32[]{:S(2)}) copy-start(f32[32,768]{1,0:T(8,128)} %get-tuple-element.737) | copy-start | bytes 294916 | tf_op jit(solution)/shard_map/while
  2511.7 66.7 %copy-start.18 = (s32[2,768]{1,0:T(2,128)S(1)}, s32[2,768]{1,0:T(2,128)}, u32[]{:S(2)}) copy-start(s32[2,768]{1,0:T(2,128)} %get-tuple-element.857) | copy-start | bytes 18436 | tf_op jit(solution)/shard_map/while
  2578.3 138.7 %collective-permute-start = (bf16[1536,32,128]{2,0,1:T(8,128)(2,1)}, bf16[1536,32,128]{2,0,1:T(8,128)(2,1)}, u32[]{:S(2)}, u32[]{:S(2)}) collective-permute-start(bf16[1536,32,128]{2,0,1:T(8,128)(2,1)} %get-tuple-element.801), channel_id=1, source_target_pairs={{0,1},{1,2},{2,3},{3,4},{4,5},{5,6},{6,7},{7,0}} | collective-permute-start | bytes 37748744 | tf_op jit(solution)/shard_map/while/body/eval_jaxpr/ppermute | solution.py:95
  2578.3 358.9 %collective-permute-start.1 = (bf16[1536,32,128]{2,0,1:T(8,128)(2,1)}, bf16[1536,32,128]{2,0,1:T(8,128)(2,1)}, u32[]{:S(2)}, u32[]{:S(2)}) collective-permute-start(bf16[1536,32,128]{2,0,1:T(8,128)(2,1)} %get-tuple-element.802), channel_id=1, source_target_pairs={{0,1},{1,2},{2,3},{3,4},{4,5},{5,6},{6,7},{7,0}} | collective-permute-start | bytes 37748744 | tf_op jit(solution)/shard_map/while/body/eval_jaxpr/ppermute | solution.py:96
  2948.6 66.9 %copy-start.12 = (f32[32,768]{1,0:T(8,128)S(1)}, f32[32,768]{1,0:T(8,128)}, u32[]{:S(2)}) copy-start(f32[32,768]{1,0:T(8,128)} %get-tuple-element.737) | copy-start | bytes 294916 | tf_op jit(solution)/shard_map/while
  3015.5 66.7 %copy-start.18 = (s32[2,768]{1,0:T(2,128)S(1)}, s32[2,768]{1,0:T(2,128)}, u32[]{:S(2)}) copy-start(s32[2,768]{1,0:T(2,128)} %get-tuple-element.857) | copy-start | bytes 18436 | tf_op jit(solution)/shard_map/while
  3082.2 138.7 %collective-permute-start = (bf16[1536,32,128]{2,0,1:T(8,128)(2,1)}, bf16[1536,32,128]{2,0,1:T(8,128)(2,1)}, u32[]{:S(2)}, u32[]{:S(2)}) collective-permute-start(bf16[1536,32,128]{2,0,1:T(8,128)(2,1)} %get-tuple-element.801), channel_id=1, source_target_pairs={{0,1},{1,2},{2,3},{3,4},{4,5},{5,6},{6,7},{7,0}} | collective-permute-start | bytes 37748744 | tf_op jit(solution)/shard_map/while/body/eval_jaxpr/ppermute | solution.py:95
  3082.2 358.9 %collective-permute-start.1 = (bf16[1536,32,128]{2,0,1:T(8,128)(2,1)}, bf16[1536,32,128]{2,0,1:T(8,128)(2,1)}, u32[]{:S(2)}, u32[]{:S(2)}) collective-permute-start(bf16[1536,32,128]{2,0,1:T(8,128)(2,1)} %get-tuple-element.802), channel_id=1, source_target_pairs={{0,1},{1,2},{2,3},{3,4},{4,5},{5,6},{6,7},{7,0}} | collective-permute-start | bytes 37748744 | tf_op jit(solution)/shard_map/while/body/eval_jaxpr/ppermute | solution.py:96
  3452.4 66.9 %copy-start.12 = (f32[32,768]{1,0:T(8,128)S(1)}, f32[32,768]{1,0:T(8,128)}, u32[]{:S(2)}) copy-start(f32[32,768]{1,0:T(8,128)} %get-tuple-element.737) | copy-start | bytes 294916 | tf_op jit(solution)/shard_map/while
  3519.3 66.7 %copy-start.18 = (s32[2,768]{1,0:T(2,128)S(1)}, s32[2,768]{1,0:T(2,128)}, u32[]{:S(2)}) copy-start(s32[2,768]{1,0:T(2,128)} %get-tuple-element.857) | copy-start | bytes 18436 | tf_op jit(solution)/shard_map/while
  3586.0 138.7 %collective-permute-start = (bf16[1536,32,128]{2,0,1:T(8,128)(2,1)}, bf16[1536,32,128]{2,0,1:T(8,128)(2,1)}, u32[]{:S(2)}, u32[]{:S(2)}) collective-permute-start(bf16[1536,32,128]{2,0,1:T(8,128)(2,1)} %get-tuple-element.801), channel_id=1, source_target_pairs={{0,1},{1,2},{2,3},{3,4},{4,5},{5,6},{6,7},{7,0}} | collective-permute-start | bytes 37748744 | tf_op jit(solution)/shard_map/while/body/eval_jaxpr/ppermute | solution.py:95
  3586.0 358.9 %collective-permute-start.1 = (bf16[1536,32,128]{2,0,1:T(8,128)(2,1)}, bf16[1536,32,128]{2,0,1:T(8,128)(2,1)}, u32[]{:S(2)}, u32[]{:S(2)}) collective-permute-start(bf16[1536,32,128]{2,0,1:T(8,128)(2,1)} %get-tuple-element.802), channel_id=1, source_target_pairs={{0,1},{1,2},{2,3},{3,4},{4,5},{5,6},{6,7},{7,0}} | collective-permute-start | bytes 37748744 | tf_op jit(solution)/shard_map/while/body/eval_jaxpr/ppermute | solution.py:96
  3956.2 66.9 %copy-start.12 = (f32[32,768]{1,0:T(8,128)S(1)}, f32[32,768]{1,0:T(8,128)}, u32[]{:S(2)}) copy-start(f32[32,768]{1,0:T(8,128)} %get-tuple-element.737) | copy-start | bytes 294916 | tf_op jit(solution)/shard_map/while
  4023.1 66.7 %copy-start.18 = (s32[2,768]{1,0:T(2,128)S(1)}, s32[2,768]{1,0:T(2,128)}, u32[]{:S(2)}) copy-start(s32[2,768]{1,0:T(2,128)} %get-tuple-element.857) | copy-start | bytes 18436 | tf_op jit(solution)/shard_map/while
  4089.8 138.7 %collective-permute-start = (bf16[1536,32,128]{2,0,1:T(8,128)(2,1)}, bf16[1536,32,128]{2,0,1:T(8,128)(2,1)}, u32[]{:S(2)}, u32[]{:S(2)}) collective-permute-start(bf16[1536,32,128]{2,0,1:T(8,128)(2,1)} %get-tuple-element.801), channel_id=1, source_target_pairs={{0,1},{1,2},{2,3},{3,4},{4,5},{5,6},{6,7},{7,0}} | collective-permute-start | bytes 37748744 | tf_op jit(solution)/shard_map/while/body/eval_jaxpr/ppermute | solution.py:95
  4089.8 358.9 %collective-permute-start.1 = (bf16[1536,32,128]{2,0,1:T(8,128)(2,1)}, bf16[1536,32,128]{2,0,1:T(8,128)(2,1)}, u32[]{:S(2)}, u32[]{:S(2)}) collective-permute-start(bf16[1536,32,128]{2,0,1:T(8,128)(2,1)} %get-tuple-element.802), channel_id=1, source_target_pairs={{0,1},{1,2},{2,3},{3,4},{4,5},{5,6},{6,7},{7,0}} | collective-permute-start | bytes 37748744 | tf_op jit(solution)/shard_map/while/body/eval_jaxpr/ppermute | solution.py:96
  4460.0 66.9 %copy-start.12 = (f32[32,768]{1,0:T(8,128)S(1)}, f32[32,768]{1,0:T(8,128)}, u32[]{:S(2)}) copy-start(f32[32,768]{1,0:T(8,128)} %get-tuple-element.737) | copy-start | bytes 294916 | tf_op jit(solution)/shard_map/while
  4527.0 66.7 %copy-start.18 = (s32[2,768]{1,0:T(2,128)S(1)}, s32[2,768]{1,0:T(2,128)}, u32[]{:S(2)}) copy-start(s32[2,768]{1,0:T(2,128)} %get-tuple-element.857) | copy-start | bytes 18436 | tf_op jit(solution)/shard_map/while
  4593.6 138.7 %collective-permute-start = (bf16[1536,32,128]{2,0,1:T(8,128)(2,1)}, bf16[1536,32,128]{2,0,1:T(8,128)(2,1)}, u32[]{:S(2)}, u32[]{:S(2)}) collective-permute-start(bf16[1536,32,128]{2,0,1:T(8,128)(2,1)} %get-tuple-element.801), channel_id=1, source_target_pairs={{0,1},{1,2},{2,3},{3,4},{4,5},{5,6},{6,7},{7,0}} | collective-permute-start | bytes 37748744 | tf_op jit(solution)/shard_map/while/body/eval_jaxpr/ppermute | solution.py:95
  4593.6 358.9 %collective-permute-start.1 = (bf16[1536,32,128]{2,0,1:T(8,128)(2,1)}, bf16[1536,32,128]{2,0,1:T(8,128)(2,1)}, u32[]{:S(2)}, u32[]{:S(2)}) collective-permute-start(bf16[1536,32,128]{2,0,1:T(8,128)(2,1)} %get-tuple-element.802), channel_id=1, source_target_pairs={{0,1},{1,2},{2,3},{3,4},{4,5},{5,6},{6,7},{7,0}} | collective-permute-start | bytes 37748744 | tf_op jit(solution)/shard_map/while/body/eval_jaxpr/ppermute | solution.py:96
  4963.8 66.9 %copy-start.12 = (f32[32,768]{1,0:T(8,128)S(1)}, f32[32,768]{1,0:T(8,128)}, u32[]{:S(2)}) copy-start(f32[32,768]{1,0:T(8,128)} %get-tuple-element.737) | copy-start | bytes 294916 | tf_op jit(solution)/shard_map/while
  5030.8 66.7 %copy-start.18 = (s32[2,768]{1,0:T(2,128)S(1)}, s32[2,768]{1,0:T(2,128)}, u32[]{:S(2)}) copy-start(s32[2,768]{1,0:T(2,128)} %get-tuple-element.857) | copy-start | bytes 18436 | tf_op jit(solution)/shard_map/while
  5521.2 161.3 %copy-start.1 = (bf16[16,64,1024]{2,1,0:T(8,128)(2,1)S(1)}, bf16[16,64,1024]{2,1,0:T(8,128)(2,1)}, u32[]{:S(2)}) copy-start(bf16[16,64,1024]{2,1,0:T(8,128)(2,1)} %param.35) | copy-start | bytes 6291460
  (59 other events, 1606.6 us)
where the time goes:
time: 5700 us; the launch traced here: 5680 us
  matrix products  2870 us (50%)
  waiting for transfers between devices  1280 us (22%)
  other arithmetic  947 us (17%)
  local copies, waits for them, and re-layouts  561 us (10%)
    dot_general x16, matrix products, attend_block(): jnp.einsum('hgqk,khd->hgqd', exp_scores.astype(jnp.bfloat16), value_blk,...  1070 us
    ppermute x7, waiting for transfers between devices, kv_step(): key_blk = lax.ppermute(key_blk, 'sp', shift_pairs)  959 us
    dot_general x16, matrix products, attend_block(): jnp.einsum('qhgd,khd->hgqk', queries, key_blk, preferred_element_type=jnp...  900 us
    reduce_sum x16, other arithmetic, attend_block(): new_sum = run_sum * factor + exp_scores.sum(axis=-1)  740 us
    all_to_all x1, waiting for transfers between devices, local_program(): recv_rows = lax.all_to_all(send_rows, 'sp', 0, 0, tiled=True)  316 us
    dynamic_update_slice x8, local copies, waits for them, and re-layouts, place(): lax.dynamic_update_slice(hidden, jnp.where(is_valid, incoming, current),...  188 us
    dot_general x1, matrix products, decoder_layer(): up_proj = jnp.dot(normed_mlp, w_up, preferred_element_type=jnp.float32)  170 us
    while x140, local copies, waits for them, and re-layouts  167 us
  transfers between devices with their start and end apart: 16, of which 8 were waited for; matrix products, arithmetic and copies ran while one was open for 32% of the time, Pallas kernels for 0%

commit v1 on v0

v1 whole, which is shorter than its diff:
```python
import functools

import jax
import jax.numpy as jnp
from jax import lax
from jax.experimental import pallas as pl
from jax.experimental.pallas import tpu as pltpu
from jax.sharding import PartitionSpec as P

ROPE_BASE = 10000.0
RMS_EPS = 1e-6
LN_EPS = 1e-5
C = (128 ** -0.5) * 1.4426950408889634
TQ, TK = 1024, 512
NEG = -1e30
BL = 768
HALF = 8 * BL
f32 = jnp.float32
bf16 = jnp.bfloat16


def layer_norm(values, gain):
    wide = values.astype(f32)
    centered = wide - wide.mean(-1, keepdims=True)
    row_var = (centered * centered).mean(-1, keepdims=True)
    return (centered * lax.rsqrt(row_var + LN_EPS) * gain.astype(f32)).astype(bf16)


def rms_norm(values, gain):
    wide = values.astype(f32)
    mean_sq = (wide * wide).mean(-1, keepdims=True)
    return (wide * lax.rsqrt(mean_sq + RMS_EPS) * gain.astype(f32)).astype(bf16)


def dot(a, b):
    return jnp.dot(a, b, preferred_element_type=f32)


def encode_image(pixels, w_patch, pos_table, ln1, w_vqkv, w_vout, ln2, w_fc1, w_fc2, w_proj1, w_proj2):
    embedded = (dot(pixels, w_patch) + pos_table.astype(f32)).astype(bf16)
    normed = layer_norm(embedded, ln1)
    qkv = jnp.einsum('pv,vthd->thpd', normed, w_vqkv, preferred_element_type=f32).astype(bf16)
    scores = jnp.einsum('hqd,hkd->hqk', qkv[0], qkv[1], preferred_element_type=f32) * w_vqkv.shape[3] ** -0.5
    prob = jax.nn.softmax(scores, axis=-1).astype(bf16)
    context = jnp.einsum('hqk,hkd->hqd', prob, qkv[2], preferred_element_type=f32).astype(bf16)
    hidden = (embedded.astype(f32) + jnp.einsum('hqd,hdv->qv', context, w_vout, preferred_element_type=f32)).astype(bf16)
    act = jax.nn.gelu(dot(layer_norm(hidden, ln2), w_fc1)).astype(bf16)
    vision = (hidden.astype(f32) + dot(act, w_fc2)).astype(bf16)
    mid = jax.nn.gelu(dot(vision, w_proj1)).astype(bf16)
    return dot(mid, w_proj2).astype(bf16)


def rope_tables():
    half = 64
    inv_freq = ROPE_BASE ** (-jnp.arange(half).astype(f32) * 2.0 / 128)
    ang = jnp.arange(2 * HALF).astype(f32)[:, None] * inv_freq[None]
    c, s = jnp.cos(ang), jnp.sin(ang)
    return jnp.concatenate([c, c], 1), jnp.concatenate([-s, s], 1)


def _colmax(s): return jnp.max(s,axis=0,keepdims=True)
def _colsum8(p): return jnp.sum(p.reshape(p.shape[0]//8,8,p.shape[1]),axis=0)

def attn_kernel(mode, *refs):
    causal = mode != 'B1'
    if mode=='A':
        q_ref,k_ref,v_ref,cq,sq,o_ref,qT,ks,vT,s0,s1,acc=refs; ck,sk=cq,sq
    elif mode=='B1':
        q_ref,k_ref,v_ref,cq,sq,ck,sk,oa_ref,oml_ref,qT,ks,vT,s0,s1,acc=refs
    else:
        q_ref,k_ref,v_ref,cq,sq,ia_ref,iml_ref,o_ref,qT,ks,vT,s0,s1,acc=refs; ck,sk=cq,sq
    sb=(s0,s1)
    def A(x): return pl.multiple_of(x,TK)
    def rope(x,cos,sin):
        xf=x.astype(f32)
        return (xf*cos+pltpu.roll(xf,64,1)*sin).astype(bf16)
    def prep(b,_):
        kb = 7-b if mode=='B2' else b
        qb = b if mode=='A' else 7-b
        r=pl.multiple_of(kb*BL,BL)
        ks[pl.ds(r,BL),:]=rope(k_ref[b,0],ck[pl.ds(r,BL),:],sk[pl.ds(r,BL),:])
        vT[:,pl.ds(r,BL)]=v_ref[b,0].T
        rq=pl.multiple_of(qb*BL,BL)
        qr=rope(q_ref[b,0],cq[pl.ds(rq,BL),:],sq[pl.ds(rq,BL),:]).astype(f32)*C
        hi=qr.astype(bf16); lo=(qr-hi.astype(f32)).astype(bf16)
        qT[0:128,pl.ds(rq,BL)]=hi.T
        qT[128:256,pl.ds(rq,BL)]=lo.T
        return 0
    lax.fori_loop(0,8,prep,0)

    def S1(j,buf,c0,w=TQ,o=0,mx=True):
        k=ks[pl.ds(j,TK),:]
        s=jnp.dot(jnp.concatenate([k,k],axis=1),qT[:,pl.ds(c0,w)],preferred_element_type=f32)
        buf[:,o:o+w]=s
        return _colmax(s) if mx else None
    def S23(j,buf,m,l,mt,mask=None,o=0,w=TQ):
        s=buf[:,o:o+w]
        if mask is not None:
            s=jnp.where(mask,s,NEG)
            mt=_colmax(s)
        mn=mt if m is None else jnp.maximum(m,mt)
        p=jnp.exp2(s-mn)
        ps=_colsum8(p)
        pv=jnp.dot(vT[:,pl.ds(j,TK)],p.astype(bf16),preferred_element_type=f32)
        if m is None:
            acc[:,o:o+w]=pv
            return mn,ps
        al=jnp.exp2(m-mn)
        acc[:,o:o+w]=acc[:,o:o+w]*al+pv
        return mn,l*al+ps
    H2=TQ-TK
    def finish(i,l):
        ls=jnp.sum(l,axis=0,keepdims=True)
        o=(acc[...]*(1.0/ls)).astype(bf16)
        for u in range(TQ//256):
            pc=i*(TQ//256)+u
            blk=pc//3; off=pl.multiple_of((pc%3)*256,256)
            if mode=='B2': blk=7-blk
            o_ref[blk,pl.ds(off,256),:]=o[:,u*256:(u+1)*256].T
    def tail(c0,d0,m,l):
        rows=lax.broadcasted_iota(jnp.int32,(TK,TQ),0); cols=lax.broadcasted_iota(jnp.int32,(TK,TQ),1)
        mk=rows<=cols
        S1(A(d0+TK),sb[1],A(c0+TK),w=H2,o=TK,mx=False)
        m,l=S23(d0,sb[0],m,l,None,mask=mk)
        m2,l2=S23(A(d0+TK),sb[1],m[:,TK:],l[:,TK:],None,mask=mk[:,:H2],o=TK,w=H2)
        return jnp.concatenate([l[:,:TK],l2],axis=1)
    def init(c0):
        if mode=='B2':
            acc[...]=ia_ref[0,:,pl.ds(c0,TQ)]
            return iml_ref[0,8:9,pl.ds(c0,TQ)],iml_ref[0,0:8,pl.ds(c0,TQ)]
        acc[...]=jnp.zeros((128,TQ),f32)
        return jnp.full((1,TQ),NEG,f32),jnp.zeros((8,TQ),f32)
    def pair(j,c,c0,last=False):
        m,l,mt=c
        mtn=S1(A(j+TK),sb[1],c0)
        m,l=S23(A(j),sb[0],m,l,mt)
        mt2=None if last else S1(A(j+2*TK),sb[0],c0)
        m,l=S23(A(j+TK),sb[1],m,l,mtn)
        return m,l,mt2
    def qtile(i,_):
        c0=pl.multiple_of(i*TQ,TQ)
        m,l=init(c0)
        mt0=S1(0,sb[0],c0)
        def body(t,c):
            j=4*t*TK
            return pair(j+2*TK,pair(j,c,c0),c0)
        if causal:
            n=2*i
            n4=n//4
            c=lax.fori_loop(0,n4,body,(m,l,mt0))
            m,l,mt=lax.fori_loop(2*n4,n//2,lambda t,c: pair(2*t*TK,c,c0),c)
            l=tail(c0,A(i*TQ),m,l)
            finish(i,l)
        else:
            n=HALF//TK
            c=lax.fori_loop(0,n//4-1,body,(m,l,mt0))
            c=pair((n-4)*TK,c,c0)
            m,l,_u=pair((n-2)*TK,c,c0,last=True)
            oa_ref[0,:,pl.ds(c0,TQ)]=acc[...]
            oml_ref[0,0:8,pl.ds(c0,TQ)]=l
            oml_ref[0,8:16,pl.ds(c0,TQ)]=jnp.broadcast_to(m,(8,TQ))
        return 0
    nq=HALF//TQ
    if causal:
        if mode=='B2': m,l=init(0)
        else: m,l=None,None
        S1(0,sb[0],0,mx=False)
        l=tail(0,0,m,l)
        finish(0,l)
        lax.fori_loop(1,nq,qtile,0)
    else:
        lax.fori_loop(0,nq,qtile,0)

def attn_call(mode,q,k,v,tabs,state=None):
    H=q.shape[1]
    bs=pl.BlockSpec((8,1,BL,128),lambda h:(0,h,0,0))
    ts=pl.BlockSpec((HALF,128),lambda h:(0,0),pipeline_mode=pl.Buffered(1))
    sa=pl.BlockSpec((1,128,HALF),lambda h:(h,0,0)); sml=pl.BlockSpec((1,16,HALF),lambda h:(h,0,0))
    ins=[q,k,v,*tabs]; in_specs=[bs]*3+[ts]*len(tabs)
    units=HALF*HALF*H*(1 if mode=='B1' else 0.55)
    by=3*q.size*2+8*BL*128*2*H
    if mode=='B2':
        ins+=list(state); in_specs+=[sa,sml]
    if mode=='B1':
        out_shape=(jax.ShapeDtypeStruct((H,128,HALF),f32),jax.ShapeDtypeStruct((H,16,HALF),f32)); out_specs=(sa,sml)
    else:
        out_shape=jax.ShapeDtypeStruct((8,BL,H*128),bf16); out_specs=pl.BlockSpec((8,BL,128),lambda h:(0,0,h))
    return pl.pallas_call(functools.partial(attn_kernel,mode),grid=(H,),in_specs=in_specs,out_specs=out_specs,out_shape=out_shape,
        scratch_shapes=[pltpu.VMEM((256,HALF),bf16),pltpu.VMEM((HALF,128),bf16),pltpu.VMEM((128,HALF),bf16),
            pltpu.VMEM((TK,TQ),f32),pltpu.VMEM((TK,TQ),f32),pltpu.VMEM((128,TQ),f32)],
        compiler_params=pltpu.CompilerParams(dimension_semantics=("arbitrary",),vmem_limit_bytes=56<<20),
        cost_estimate=pl.CostEstimate(flops=int(1100*units),bytes_accessed=by,transcendentals=int(units)),
        name="attn_"+mode)(*ins)


def after(x, *deps):
    return lax.optimization_barrier((x,) + deps)[0]


def route_patches(pixels, starts, me):
    blk = starts // BL
    everyone = lax.all_gather(pixels, 'sp', axis=0, tiled=True)
    order = jnp.arange(16)
    picks = []
    for mine in (me, 15 - me):
        hit = blk == mine
        picks.append(lax.dynamic_index_in_dim(everyone, jnp.sum(jnp.where(hit, order, 0)), keepdims=False))
        picks.append(jnp.sum(jnp.where(hit, starts % BL, 0)))
    return picks


def exchange(x):
    return lax.all_to_all(x, 'sp', 0, 0, tiled=True)


def solution(mesh):
    def local_program(x_rows, pixels, starts, w_patch, pos_table, vit_ln1, w_vqkv, w_vout, vit_ln2, w_fc1, w_fc2, w_proj1, w_proj2, rms_attn, w_query, w_key, w_value, w_out, rms_mlp, w_gate, w_up, w_down):
        me = lax.axis_index('sp')
        px_a, off_a, px_b, off_b = route_patches(pixels, starts, me)
        cos, sin = rope_tables()
        tab_a, tab_b = (cos[:HALF], sin[:HALF]), (cos[HALF:], sin[HALF:])
        enc = lambda px: encode_image(px, w_patch, pos_table, vit_ln1, w_vqkv, w_vout, vit_ln2, w_fc1, w_fc2, w_proj1, w_proj2)
        w_out2 = w_out.reshape(8, 512, 4096)

        def place(rows, img, off):
            h0 = lax.dynamic_update_slice(rows, img, (off, 0))
            return h0, rms_norm(h0, rms_attn)

        def project(n1, w):
            y = jnp.einsum('sd,dhe->hse', n1, w, preferred_element_type=f32).astype(bf16)
            return exchange(y.reshape(8, 4, BL, 128))

        def finish(ctx, h0):
            mid = (h0.astype(f32) + jnp.einsum('sqc,scd->qd', ctx, w_out2, preferred_element_type=f32)).astype(bf16)
            n2 = rms_norm(mid, rms_mlp)
            y = (jax.nn.silu(dot(n2, w_gate)) * dot(n2, w_up)).astype(bf16)
            return (mid.astype(f32) + dot(y, w_down)).astype(bf16)

        h0a, n1a = place(x_rows[:BL], enc(px_a), off_a)
        ka, va, qa = project(n1a, w_key), project(n1a, w_value), project(n1a, w_query)
        h0b, n1b = place(x_rows[BL:], enc(px_b), off_b)
        qb, kb, vb = project(n1b, w_query), project(n1b, w_key), project(n1b, w_value)
        ctx_a = exchange(attn_call('A', qa, ka, va, tab_a))
        state = attn_call('B1', qb, ka, va, tab_b + tab_a)
        ctx_b = exchange(attn_call('B2', qb, kb, vb, tab_b, state))
        out_a = finish(ctx_a, h0a)
        out_b = finish(ctx_b, h0b)
        return jnp.concatenate([out_a, out_b], axis=0)

    row_spec = P(('dp', 'sp'), None)
    in_specs = (row_spec, P(('dp', 'sp'), None, None), P('dp')) + (P(),) * 19
    return jax.shard_map(local_program, mesh=mesh, in_specs=in_specs, out_specs=row_spec, check_vma=False)
```

time: 5700 us -> 1700 us (0.30)
  matrix products: 2870 us -> 924 us
  waiting for transfers between devices: 1280 us -> 161 us
  other arithmetic: 947 us -> 73.2 us
  local copies, waits for them, and re-layouts: 561 us -> 60.7 us
  Pallas kernels: 0 us -> 420 us
    dot_general x44 -> x24, matrix products: 2730 us -> 887 us  [the longest x14 599 us: dot(): return jnp.dot(a, b, preferred_element_type=f32)]
    ppermute x14 -> x0, waiting for transfers between devices: 959 us -> none  [the longest x7 959 us: kv_step(): key_blk = lax.ppermute(key_blk, 'sp', shift_pairs)]
    reduce_sum x18 -> x1, other arithmetic: 740 us -> 1.37 us  [route_patches(): picks.append(jnp.sum(jnp.where(hit, starts % BL, 0)))]
    pallas_call x0 -> x3, Pallas kernels: none -> 420 us  [attn_call(): pl.pallas_call(functools.partial(attn_kernel, mode), grid=(H,), in_specs=...]
    while x141 -> x0, local copies, waits for them, and re-layouts: 183 us -> none
    all_to_all x2 -> x8, waiting for transfers between devices: 316 us -> 151 us  [exchange(): return lax.all_to_all(x, 'sp', 0, 0, tiled=True)]
    dynamic_update_slice x10 -> x2, local copies, waits for them, and re-layouts: 198 us -> 46.9 us  [place(): h0 = lax.dynamic_update_slice(rows, img, (off, 0))]
    unnamed x2, matrix products: 125 us -> 11.1 us
  transfers between devices with their start and end apart: 16 -> 9, of which waited for: 8 -> 5; matrix products, arithmetic and copies ran while one was open for 32% -> 21% of each run, Pallas kernels for 0% -> 25%
where the time goes in v1:
time: 1700 us; the launch traced here: 1690 us
  matrix products  924 us (54%)
  Pallas kernels  420 us (25%)
  waiting for transfers between devices  161 us (9%)
  other arithmetic  73.2 us (4%)
  local copies, waits for them, and re-layouts  60.7 us (4%)
  starting transfers between devices  29.5 us (2%)
  between operations  21.6 us (1%)
    dot_general x14, matrix products, dot(): return jnp.dot(a, b, preferred_element_type=f32)  599 us
    pallas_call x3, Pallas kernels, attn_call(): pl.pallas_call(functools.partial(attn_kernel, mode), grid=(H,), in_specs=...  420 us
    dot_general x6, matrix products, project(): jnp.einsum('sd,dhe->hse', n1, w, preferred_element_type=f32).astype(bf16)  198 us
    all_to_all x8, waiting for transfers between devices, exchange(): return lax.all_to_all(x, 'sp', 0, 0, tiled=True)  151 us
    dot_general x2, matrix products, finish(): jnp.einsum('sqc,scd->qd', ctx, w_out2, preferred_element_type=f32)  66.9 us
    dynamic_update_slice x2, local copies, waits for them, and re-layouts, place(): h0 = lax.dynamic_update_slice(rows, img, (off, 0))  46.9 us
  transfers between devices with their start and end apart: 9, of which 5 were waited for; matrix products, arithmetic and copies ran while one was open for 21% of the time, Pallas kernels for 25%

profile of v1, /device:TPU:0, one launch (start us, length us, event | category | flops | bytes accessed | tf_op | source)
XLA Modules:
  0.0 1690.0 jit_solution(3598876420990473188)
XLA Ops:
  19.0 25.4 %fusion.153 = (f32[12288,64]{1,0:T(8,128)S(1)}, f32[12288,64]{1,0:T(8,128)S(1)}, f32[12288,64]{1,0:T(8,128)}) fusion(f32[64]{0:T(128)S(1)} %multiply_power_fusion, f32[12288]{0:T(1024)S(1)} %iota_convert_fusion), kind=kLoop, calls=%fused_computation.175 | loop fusion | flops 1572864 | bytes 9486592 | tf_op jit(solution)/shard_map/neg | solution.py:58
  98.4 12.9 fusion.220
  124.6 17.5 %fusion.150 = bf16[576,1024]{1,0:T(8,128)(2,1)} fusion(bf16[576,1024]{1,0:T(8,128)(2,1)} %get-tuple-element.33, bf16[4096,1024]{1,0:T(8,128)(2,1)} %param.32, bf16[1024,4096]{1,0:T(8,128)(2,1)} %param.31, f32[1024]{0:T(1024)S(1)} %convert_element_type.227, f32[576]{0:T(1024)S(1)} %add_rsqrt_fusion.6, f32[576]{0:T(1024)S(1)} %broadcast_multiply_fusion.2), kind=kOutput, calls=%fused_computation.172 | convolution fusion | flops 9689628672 | bytes 19145216 | tf_op jit(solution)/shard_map/dot_general | solution.py:36
  151.7 24.8 %convolution_convert_fusion.1 = bf16[576,4096]{1,0:T(8,128)(2,1)} fusion(bf16[4096,4096]{1,0:T(8,128)(2,1)} %param.34, bf16[576,4096]{1,0:T(8,128)(2,1)S(1)} %fusion.316), kind=kOutput, calls=%fused_computation.109 | convolution fusion | flops 19329712128 | bytes 42991616 | tf_op jit(solution)/shard_map/dot_general | solution.py:36
  176.4 23.5 %dynamic_update_slice.6 = bf16[768,4096]{1,0:T(8,128)(2,1)} dynamic-update-slice(bf16[768,4096]{1,0:T(8,128)(2,1)} %get-tuple-element.15, bf16[576,4096]{1,0:T(8,128)(2,1)} %convolution_convert_fusion.1, s32[]{:T(128)S(6)} %select_n.45, s32[]{:T(128)} %constant.64.clone.1) | dynamic-update-slice | bytes 9437188 | tf_op jit(solution)/shard_map/dynamic_update_slice | solution.py:226
  204.5 31.5 %fusion.109 = bf16[768,32,128]{2,0,1:T(8,128)(2,1)} fusion(bf16[4096,32,128]{2,1,0:T(8,128)(2,1)} %param.37, bf16[768,4096]{1,0:T(8,128)(2,1)S(1)} %copy-done.2, f32[4096]{0:T(1024)S(1)} %copy-done.5, f32[768]{0:T(1024)S(1)} %add_rsqrt_fusion.5), kind=kOutput, calls=%fused_computation.137 | convolution fusion | flops 25785532416 | bytes 46156800 | tf_op jit(solution)/shard_map/sd,dhe->hse/dot_general | solution.py:230
  239.9 33.3 %fusion.115 = bf16[768,32,128]{2,0,1:T(8,128)(2,1)} fusion(bf16[4096,32,128]{2,1,0:T(8,128)(2,1)} %param.38, bf16[768,4096]{1,0:T(8,128)(2,1)} %dynamic_update_slice.6, f32[4096]{0:T(1024)S(1)} %copy-done.5, f32[768]{0:T(1024)S(1)} %add_rsqrt_fusion.5), kind=kOutput, calls=%fused_computation.139 | convolution fusion | flops 25785532416 | bytes 46156800 | tf_op jit(solution)/shard_map/sd,dhe->hse/dot_general | solution.py:230
  273.2 13.0 fusion.219
  286.2 11.5 convert_reduce_fusion
  299.5 16.5 fusion.152
  326.8 24.8 %convolution_convert_fusion = bf16[576,4096]{1,0:T(8,128)(2,1)} fusion(bf16[4096,4096]{1,0:T(8,128)(2,1)} %param.34, bf16[576,4096]{1,0:T(8,128)(2,1)S(1)} %fusion.312), kind=kOutput, calls=%fused_computation.108 | convolution fusion | flops 19329712128 | bytes 42991616 | tf_op jit(solution)/shard_map/dot_general | solution.py:36
  351.6 23.4 %dynamic_update_slice.7 = bf16[768,4096]{1,0:T(8,128)(2,1)} dynamic-update-slice(bf16[768,4096]{1,0:T(8,128)(2,1)} %get-tuple-element.16, bf16[576,4096]{1,0:T(8,128)(2,1)} %convolution_convert_fusion, s32[]{:T(128)S(6)} %select_n.49, s32[]{:T(128)} %constant.64.clone.1) | dynamic-update-slice | bytes 9437188 | tf_op jit(solution)/shard_map/dynamic_update_slice | solution.py:226
  379.1 33.4 %fusion.103 = bf16[768,32,128]{2,0,1:T(8,128)(2,1)} fusion(bf16[4096,32,128]{2,1,0:T(8,128)(2,1)} %param.36, bf16[768,4096]{1,0:T(8,128)(2,1)} %dynamic_update_slice.6, f32[4096]{0:T(1024)S(1)} %copy-done.5, f32[768]{0:T(1024)S(1)} %add_rsqrt_fusion.5), kind=kOutput, calls=%fused_computation.135 | convolution fusion | flops 25785532416 | bytes 46156800 | tf_op jit(solution)/shard_map/sd,dhe->hse/dot_general | solution.py:230
  416.5 33.2 %fusion.112 = bf16[768,32,128]{2,0,1:T(8,128)(2,1)} fusion(bf16[4096,32,128]{2,1,0:T(8,128)(2,1)} %param.37, bf16[768,4096]{1,0:T(8,128)(2,1)} %dynamic_update_slice.7, f32[768]{0:T(1024)S(1)} %add_rsqrt_fusion.1, f32[4096]{0:T(1024)S(1)} %copy-done.5), kind=kOutput, calls=%fused_computation.138 | convolution fusion | flops 25785532416 | bytes 46156800 | tf_op jit(solution)/shard_map/sd,dhe->hse/dot_general | solution.py:230
  449.7 38.3 %all-to-all-done.2.refs_2_ = bf16[8,4,768,128]{3,2,1,0:T(8,128)(2,1)} async-done(((bf16[8,4,768,128]{3,2,1,0:T(8,128)(2,1)}), bf16[8,4,768,128]{3,2,1,0:T(8,128)(2,1)}, u32[]{:S(2)}, u32[]{:S(2)}) %all-to-all-start.2) | async-done | bytes 6291488 | tf_op jit(solution)/shard_map/all_to_all | solution.py:213
  491.5 33.4 %fusion.106 = bf16[768,32,128]{2,0,1:T(8,128)(2,1)} fusion(bf16[4096,32,128]{2,1,0:T(8,128)(2,1)} %param.36, bf16[768,4096]{1,0:T(8,128)(2,1)} %dynamic_update_slice.7, f32[768]{0:T(1024)S(1)} %add_rsqrt_fusion.1, f32[4096]{0:T(1024)S(1)} %copy-done.5), kind=kOutput, calls=%fused_computation.136 | convolution fusion | flops 25785532416 | bytes 46156800 | tf_op jit(solution)/shard_map/sd,dhe->hse/dot_general | solution.py:230
  524.9 38.1 %all-to-all-done.refs_0_ = bf16[8,4,768,128]{3,2,1,0:T(8,128)(2,1)} async-done(((bf16[8,4,768,128]{3,2,1,0:T(8,128)(2,1)}), bf16[8,4,768,128]{3,2,1,0:T(8,128)(2,1)}, u32[]{:S(2)}, u32[]{:S(2)}) %all-to-all-start) | async-done | bytes 6291488 | tf_op jit(solution)/shard_map/all_to_all | solution.py:213
  566.6 33.3 %fusion.118 = bf16[768,32,128]{2,0,1:T(8,128)(2,1)} fusion(bf16[4096,32,128]{2,1,0:T(8,128)(2,1)} %param.38, bf16[768,4096]{1,0:T(8,128)(2,1)} %dynamic_update_slice.7, f32[768]{0:T(1024)S(1)} %add_rsqrt_fusion.1, f32[4096]{0:T(1024)S(1)} %copy-done.5), kind=kOutput, calls=%fused_computation.140 | convolution fusion | flops 25785532416 | bytes 46156800 | tf_op jit(solution)/shard_map/sd,dhe->hse/dot_general | solution.py:230
  599.9 38.2 %all-to-all-done.4.refs_0_ = bf16[8,4,768,128]{3,2,1,0:T(8,128)(2,1)} async-done(((bf16[8,4,768,128]{3,2,1,0:T(8,128)(2,1)}), bf16[8,4,768,128]{3,2,1,0:T(8,128)(2,1)}, u32[]{:S(2)}, u32[]{:S(2)}) %all-to-all-start.4) | async-done | bytes 6291488 | tf_op jit(solution)/shard_map/all_to_all | solution.py:213
  641.6 186.0 %attn_B1.1 = (f32[4,128,6144]{2,1,0:T(8,128)}, f32[4,16,6144]{2,1,0:T(8,128)}) custom-call(bf16[8,4,768,128]{3,2,1,0:T(8,128)(2,1)} %all-to-all-done.4.refs_0_, bf16[8,4,768,128]{3,2,1,0:T(8,128)(2,1)} %all-to-all-done.1.refs_1_, bf16[8,4,768,128]{3,2,1,0:T(8,128)(2,1)} %all-to-all-done.2.refs_2_, f32[6144,128]{1,0:T(8,128)} %get-tuple-element.38.refs_3_, ...), custom_call_target="tpu_custom_call" | custom-call | flops 166094438400 | bytes 25165824 | tf_op jit(solution)/shard_map/attn_B1/pallas_call | solution.py:188
  831.3 115.8 %attn_A.1 = bf16[8,768,512]{2,1,0:T(8,128)(2,1)} custom-call(bf16[8,4,768,128]{3,2,1,0:T(8,128)(2,1)} %all-to-all-done.refs_0_, bf16[8,4,768,128]{3,2,1,0:T(8,128)(2,1)} %all-to-all-done.1.refs_1_, bf16[8,4,768,128]{3,2,1,0:T(8,128)(2,1)} %all-to-all-done.2.refs_2_, f32[6144,128]{1,0:T(8,128)} %get-tuple-element.39.refs_3_.refs_5_, ...), custom_call_target="tpu_custom_call" | custom-call | flops 91351941120 | bytes 25165824 | tf_op jit(solution)/shard_map/attn_A/pallas_call | solution.py:188
  950.7 118.1 %attn_B2.1 = bf16[8,768,512]{2,1,0:T(8,128)(2,1)} custom-call(bf16[8,4,768,128]{3,2,1,0:T(8,128)(2,1)} %all-to-all-done.4.refs_0_, bf16[8,4,768,128]{3,2,1,0:T(8,128)(2,1)} %all-to-all-done.5.refs_1_, bf16[8,4,768,128]{3,2,1,0:T(8,128)(2,1)} %all-to-all-done.6.refs_2_, f32[6144,128]{1,0:T(8,128)} %get-tuple-element.38.refs_3_, ...), custom_call_target="tpu_custom_call" | custom-call | flops 91351941120 | bytes 25165824 | tf_op jit(solution)/shard_map/attn_B2/pallas_call | solution.py:188
  1072.7 34.0 %fusion.28 = (f32[768]{0:T(1024)S(1)}, bf16[768,4096]{1,0:T(8,128)(2,1)}) fusion(bf16[8,768,512]{2,1,0:T(8,128)(2,1)} %all-to-all-done.3, bf16[8,512,4096]{2,1,0:T(8,128)(2,1)} %bitcast.192, bf16[768,4096]{1,0:T(8,128)(2,1)} %dynamic_update_slice.6), kind=kOutput, calls=%fused_computation.48 | convolution fusion | flops 25788678144 | bytes 52431872 | tf_op jit(solution)/shard_map/sqc,scd->qd/dot_general | solution.py:234
  1107.3 36.9 %all-to-all-done.7 = bf16[8,768,512]{2,1,0:T(8,128)(2,1)} async-done(((bf16[8,768,512]{2,1,0:T(8,128)(2,1)}), bf16[8,768,512]{2,1,0:T(8,128)(2,1)}, u32[]{:S(2)}, u32[]{:S(2)}) %all-to-all-start.7) | async-done | bytes 6291488 | tf_op jit(solution)/shard_map/all_to_all | solution.py:213
  1144.2 32.9 %fusion.36 = (f32[768]{0:T(1024)S(1)}, bf16[768,4096]{1,0:T(8,128)(2,1)S(1)}) fusion(bf16[8,768,512]{2,1,0:T(8,128)(2,1)} %all-to-all-done.7, bf16[8,512,4096]{2,1,0:T(8,128)(2,1)} %bitcast.193, bf16[768,4096]{1,0:T(8,128)(2,1)} %dynamic_update_slice.7), kind=kOutput, calls=%fused_computation.56 | convolution fusion | flops 25788678144 | bytes 52431872 | tf_op jit(solution)/shard_map/sqc,scd->qd/dot_general | solution.py:234
  1179.8 79.6 %fusion.87 = f32[768,11008]{1,0:T(8,128)} fusion(bf16[4096,11008]{1,0:T(8,128)(2,1)} %param.41, bf16[768,4096]{1,0:T(8,128)(2,1)S(1)} %get-tuple-element.35, f32[768]{0:T(1024)S(1)} %add_rsqrt_fusion, f32[4096]{0:T(1024)S(1)} %convert_element_type.246), kind=kOutput, calls=%fused_computation.110 | convolution fusion | flops 69268930560 | bytes 130305024 | tf_op jit(solution)/shard_map/dot_general | solution.py:36
  1259.4 83.7 %multiply_convert_fusion.clone.6 = bf16[768,11008]{1,0:T(8,128)(2,1)} fusion(f32[768,11008]{1,0:T(8,128)} %fusion.87, bf16[4096,11008]{1,0:T(8,128)(2,1)} %param.42, bf16[768,4096]{1,0:T(8,128)(2,1)} %copy-done.12, f32[768]{0:T(1024)S(1)} %add_rsqrt_fusion, f32[4096]{0:T(1024)S(1)} %convert_element_type.246), kind=kOutput, calls=%fused_computation.2.clone.clone.clone.clone.clone.1 | convolution fusion | flops 69319655424 | bytes 147213312 | tf_op jit(solution)/shard_map/dot_general | solution.py:36
  1343.1 80.0 %fusion.80 = f32[768,11008]{1,0:T(8,128)} fusion(bf16[4096,11008]{1,0:T(8,128)(2,1)} %param.41, bf16[768,4096]{1,0:T(8,128)(2,1)S(1)} %copy-done.11, f32[4096]{0:T(1024)S(1)} %convert_element_type.246, f32[768]{0:T(1024)S(1)} %copy-done.9), kind=kOutput, calls=%fused_computation.105 | convolution fusion | flops 69268930560 | bytes 130305024 | tf_op jit(solution)/shard_map/dot_general | solution.py:36
  1423.1 82.7 %multiply_convert_fusion.1.clone.6 = bf16[768,11008]{1,0:T(8,128)(2,1)} fusion(f32[768,11008]{1,0:T(8,128)} %fusion.80, bf16[4096,11008]{1,0:T(8,128)(2,1)} %param.42, bf16[768,4096]{1,0:T(8,128)(2,1)S(1)} %copy-done.11, f32[4096]{0:T(1024)S(1)} %convert_element_type.246, f32[768]{0:T(1024)S(1)} %copy-done.9), kind=kOutput, calls=%fused_computation.3.clone.clone.clone.clone.clone.1 | convolution fusion | flops 69319655424 | bytes 147213312 | tf_op jit(solution)/shard_map/dot_general | solution.py:36
  1505.8 81.4 %fusion.39 = bf16[768,4096]{1,0:T(8,128)(2,1)} fusion(bf16[768,4096]{1,0:T(8,128)(2,1)} %copy-done.12, bf16[11008,4096]{1,0:T(8,128)(2,1)} %param.43, bf16[768,11008]{1,0:T(8,128)(2,1)} %multiply_convert_fusion.clone.6), kind=kOutput, calls=%fused_computation.59 | convolution fusion | flops 69265784832 | bytes 119668736 | tf_op jit(solution)/shard_map/dot_general | solution.py:36
  1587.2 81.4 %fusion.31 = bf16[768,4096]{1,0:T(8,128)(2,1)} fusion(bf16[768,4096]{1,0:T(8,128)(2,1)} %get-tuple-element.37, bf16[11008,4096]{1,0:T(8,128)(2,1)} %param.43, bf16[768,11008]{1,0:T(8,128)(2,1)} %multiply_convert_fusion.1.clone.6), kind=kOutput, calls=%fused_computation.51 | convolution fusion | flops 69265784832 | bytes 119668736 | tf_op jit(solution)/shard_map/dot_general | solution.py:36
  1668.6 14.3 pad_maximum_fusion
  (82 shorter events, 135.7 us)
Async XLA Ops:
  6.5 104.8 %copy-start = (bf16[16,64,1024]{2,1,0:T(8,128)(2,1)S(1)}, bf16[16,64,1024]{2,1,0:T(8,128)(2,1)}, u32[]{:S(2)}) copy-start(bf16[16,64,1024]{2,1,0:T(8,128)(2,1)} %param.29) | copy-start | bytes 6291460
  6.5 68.4 %all-gather.2.cloned.1.call-start = ((), (), s32[]{:S(2)}) async-start(), calls=%async_computation.8 | async-start | bytes 13271040 | tf_op jit(solution)/shard_map/all_gather | solution.py:202
  15.1 109.5 %copy-start.7 = (f32[1024]{0:T(1024)}, f32[1024]{0:T(1024)S(1)}, u32[]{:S(2)}) copy-start(f32[1024]{0:T(1024)S(1)} %convert_element_type.227) | copy-start | bytes 12292
  55.5 19.5 %copy-start.10 = (bf16[576,1024]{1,0:T(8,128)(2,1)S(1)}, bf16[576,1024]{1,0:T(8,128)(2,1)}, u32[]{:S(2)}) copy-start(bf16[576,1024]{1,0:T(8,128)(2,1)} %param.26) | copy-start | bytes 3538948
  75.0 7.3 slice-start
  77.8 9.8 copy-start.3
  77.8 4.5 slice-start.1
  176.4 27.7 %copy-start.5 = (f32[4096]{0:T(1024)S(1)}, f32[4096]{0:T(1024)}, u32[]{:S(2)}) copy-start(f32[4096]{0:T(1024)} %convert_element_type.234) | copy-start | bytes 49156
  199.9 4.6 copy-start.2
  236.0 176.6 %all-to-all-start.1 = ((bf16[8,4,768,128]{3,2,1,0:T(8,128)(2,1)}), bf16[8,4,768,128]{3,2,1,0:T(8,128)(2,1)}, u32[]{:S(2)}, u32[]{:S(2)}) async-start(bf16[8,4,768,128]{3,2,1,0:T(8,128)(2,1)} %bitcast.187), calls=%async_computation.1 | async-start | bytes 12582912 | tf_op jit(solution)/shard_map/all_to_all | solution.py:213
  273.2 13.0 copy-start.4
  286.2 13.2 copy-start.8
  412.5 75.4 %all-to-all-start.2 = ((bf16[8,4,768,128]{3,2,1,0:T(8,128)(2,1)}), bf16[8,4,768,128]{3,2,1,0:T(8,128)(2,1)}, u32[]{:S(2)}, u32[]{:S(2)}) async-start(bf16[8,4,768,128]{3,2,1,0:T(8,128)(2,1)} %bitcast.186), calls=%async_computation.2 | async-start | bytes 12582912 | tf_op jit(solution)/shard_map/all_to_all | solution.py:213
  488.0 75.0 %all-to-all-start = ((bf16[8,4,768,128]{3,2,1,0:T(8,128)(2,1)}), bf16[8,4,768,128]{3,2,1,0:T(8,128)(2,1)}, u32[]{:S(2)}, u32[]{:S(2)}) async-start(bf16[8,4,768,128]{3,2,1,0:T(8,128)(2,1)} %bitcast.190), calls=%async_computation | async-start | bytes 12582912 | tf_op jit(solution)/shard_map/all_to_all | solution.py:213
  562.9 75.2 %all-to-all-start.4 = ((bf16[8,4,768,128]{3,2,1,0:T(8,128)(2,1)}), bf16[8,4,768,128]{3,2,1,0:T(8,128)(2,1)}, u32[]{:S(2)}, u32[]{:S(2)}) async-start(bf16[8,4,768,128]{3,2,1,0:T(8,128)(2,1)} %bitcast.191), calls=%async_computation.4 | async-start | bytes 12582912 | tf_op jit(solution)/shard_map/all_to_all | solution.py:213
  638.1 189.5 %all-to-all-start.5 = ((bf16[8,4,768,128]{3,2,1,0:T(8,128)(2,1)}), bf16[8,4,768,128]{3,2,1,0:T(8,128)(2,1)}, u32[]{:S(2)}, u32[]{:S(2)}) async-start(bf16[8,4,768,128]{3,2,1,0:T(8,128)(2,1)} %bitcast.188), calls=%async_computation.5 | async-start | bytes 12582912 | tf_op jit(solution)/shard_map/all_to_all | solution.py:213
  827.6 119.5 %all-to-all-start.6 = ((bf16[8,4,768,128]{3,2,1,0:T(8,128)(2,1)}), bf16[8,4,768,128]{3,2,1,0:T(8,128)(2,1)}, u32[]{:S(2)}, u32[]{:S(2)}) async-start(bf16[8,4,768,128]{3,2,1,0:T(8,128)(2,1)} %bitcast.189), calls=%async_computation.6 | async-start | bytes 12582912 | tf_op jit(solution)/shard_map/all_to_all | solution.py:213
  947.2 121.6 %all-to-all-start.3 = ((bf16[8,768,512]{2,1,0:T(8,128)(2,1)}), bf16[8,768,512]{2,1,0:T(8,128)(2,1)}, u32[]{:S(2)}, u32[]{:S(2)}) async-start(bf16[8,768,512]{2,1,0:T(8,128)(2,1)} %attn_A.1), calls=%async_computation.3 | async-start | bytes 12582912 | tf_op jit(solution)/shard_map/all_to_all | solution.py:213
  1068.8 3.9 copy-start.6
  1068.8 75.4 %all-to-all-start.7 = ((bf16[8,768,512]{2,1,0:T(8,128)(2,1)}), bf16[8,768,512]{2,1,0:T(8,128)(2,1)}, u32[]{:S(2)}, u32[]{:S(2)}) async-start(bf16[8,768,512]{2,1,0:T(8,128)(2,1)} %attn_B2.1), calls=%async_computation.7 | async-start | bytes 12582912 | tf_op jit(solution)/shard_map/all_to_all | solution.py:213
  1177.1 2.7 copy-start.12
  1259.4 83.7 %copy-start.9 = (f32[768]{0:T(1024)S(1)}, f32[768]{0:T(1024)}, u32[]{:S(2)}) copy-start(f32[768]{0:T(1024)} %add_rsqrt_fusion.4) | copy-start | bytes 9220
  1259.4 83.7 %copy-start.11 = (bf16[768,4096]{1,0:T(8,128)(2,1)S(1)}, bf16[768,4096]{1,0:T(8,128)(2,1)}, u32[]{:S(2)}) copy-start(bf16[768,4096]{1,0:T(8,128)(2,1)} %get-tuple-element.37) | copy-start | bytes 18874372
  1587.2 95.7 %copy-start.1 = (bf16[16,64,1024]{2,1,0:T(8,128)(2,1)S(1)}, bf16[16,64,1024]{2,1,0:T(8,128)(2,1)}, u32[]{:S(2)}) copy-start(bf16[16,64,1024]{2,1,0:T(8,128)(2,1)} %param.29) | copy-start | bytes 6291460
Sparse Core Ops, SparseCore 0:
  9.2 65.7 all-gather.1
